TPU v7x, 32 devices: a whole 2x2x4 slice. The times are simulated.
32 devices in a mesh: seq: 2 (over x), shard: 16 (over z, y, core).
Axes of the slice: x: 2, y: 2, z: 4, core: 2. Of those that a mesh axis runs over, the one named last changes fastest.
Arguments:
- hidden_in: bfloat16 [16, 1024, 768], P('shard', 'seq'), may hold values from -6 to 6
- encoded: bfloat16 [16, 1024, 768], P('shard', 'seq'), may hold values from -6 to 6
- cotangent: bfloat16 [16, 1024, 768], P('shard', 'seq'), may hold values from -6 to 6
- buckets: int32 [1024], replicated, may hold values from 0 to 31, as said below
- self_query: bfloat16 [768, 768], P(('seq', 'shard')), may hold values from -0.0390625 to 0.0390625
- self_key: bfloat16 [768, 768], P(('seq', 'shard')), may hold values from -0.21875 to 0.21875
- self_value: bfloat16 [768, 768], P(('seq', 'shard')), may hold values from -0.21875 to 0.21875
- self_out: bfloat16 [768, 768], P(('seq', 'shard')), may hold values from -3 to 3
- cross_query: bfloat16 [768, 768], P(('seq', 'shard')), may hold values from -0.0390625 to 0.0390625
- cross_key: bfloat16 [768, 768], P(('seq', 'shard')), may hold values from -0.21875 to 0.21875
- cross_value: bfloat16 [768, 768], P(('seq', 'shard')), may hold values from -0.21875 to 0.21875
- cross_out: bfloat16 [768, 768], P(('seq', 'shard')), may hold values from -3 to 3
- ff_gate: bfloat16 [768, 2048], P(('seq', 'shard')), may hold values from -0.21875 to 0.21875
- ff_up: bfloat16 [768, 2048], P(('seq', 'shard')), may hold values from -0.21875 to 0.21875
- ff_down: bfloat16 [2048, 768], P(('seq', 'shard')), may hold values from -0.125 to 0.125
- norm_self: bfloat16 [768], P(('seq', 'shard')), may hold values from 0.25 to 1.75
- norm_cross: bfloat16 [768], P(('seq', 'shard')), may hold values from 0.25 to 1.75
- norm_ff: bfloat16 [768], P(('seq', 'shard')), may hold values from 0.25 to 1.75
- bias_table: bfloat16 [384], P(('seq', 'shard')), may hold values from -4 to 4
Outputs:
- hidden_out: bfloat16 [16, 1024, 768], P('shard', 'seq')
- grad_hidden: bfloat16 [16, 1024, 768], P('shard', 'seq')
- grad_encoded: bfloat16 [16, 1024, 768], P('shard', 'seq')
- grad_self_query: float32 [768, 768], P(('seq', 'shard'))
- grad_self_key: float32 [768, 768], P(('seq', 'shard'))
- grad_self_value: float32 [768, 768], P(('seq', 'shard'))
- grad_self_out: float32 [768, 768], P(('seq', 'shard'))
- grad_cross_query: float32 [768, 768], P(('seq', 'shard'))
- grad_cross_key: float32 [768, 768], P(('seq', 'shard'))
- grad_cross_value: float32 [768, 768], P(('seq', 'shard'))
- grad_cross_out: float32 [768, 768], P(('seq', 'shard'))
- grad_ff_gate: float32 [768, 2048], P(('seq', 'shard'))
- grad_ff_up: float32 [768, 2048], P(('seq', 'shard'))
- grad_ff_down: float32 [2048, 768], P(('seq', 'shard'))
- grad_norm_self: float32 [768], P(('seq', 'shard'))
- grad_norm_cross: float32 [768], P(('seq', 'shard'))
- grad_norm_ff: float32 [768], P(('seq', 'shard'))
- grad_bias_table: float32 [384], P(('seq', 'shard'))
Inputs may be any that keep to these rules, and one draw needn't show every extreme that they name: `buckets`: bucket of the distance d from a key to a later query, for d = 0 to 1023: never falling as d grows, equal to d for d below 16, and 31 at the largest distance.
All inputs are finite; a program needn't handle non-finite values.
Results may differ from a plain program's by a relative error of at most 0.024.
The roundings to bfloat16 on the way count: a program that leaves them out, or rounds other values in their place, can miss the bound.
Values may be sent and summed in bfloat16 or wider, within the bound.
A program may use at most 320 MiB of HBM per device.

v0:
```python
import functools
import jax
import jax.numpy as jnp
from jax import lax
from jax.experimental import pallas as pl
from jax.experimental.pallas import tpu as pltpu
from jax.sharding import PartitionSpec as P

H = 12
BUCKETS = 32
NEGATIVE = -1e30
EPSILON = 1e-06
F32 = jnp.float32
LOW = jnp.bfloat16
PAIR = 2
TILE = 256


def contract(left, right, left_dim, right_dim):
    return lax.dot_general(
        left, right, (((left_dim,), (right_dim,)), ((), ())), preferred_element_type=F32
    )


def keep_head(value, head):
    size = value.shape[1] // PAIR
    lane = lax.broadcasted_iota(jnp.int32, value.shape, 1)
    inside = (lane >= head * size) & (lane < (head + 1) * size)
    return jnp.where(inside, value, jnp.zeros_like(value))


def toeplitz(row):
    wide = jnp.broadcast_to(row, (TILE, 2 * TILE))
    return pltpu.roll(wide, 0, 1, stride=1, stride_axis=0)[:, :TILE]


def skew_sum(total_ref):
    group = 8
    width = 2 * TILE
    summed = jnp.zeros((group, width), F32)
    for start in range(0, TILE, group):
        rows = total_ref[start : start + group, :]
        wide = jnp.concatenate([rows, jnp.zeros_like(rows)], 1)
        summed = summed + pltpu.roll(wide, (width - start) % width, 1)
    out = summed[0:1]
    for row in range(1, group):
        out = out + pltpu.roll(summed[row : row + 1], width - row, 1)
    return out


def scores_t(keys, query, tiles, last):
    scores = contract(keys, query, 1, 1)
    if tiles is None:
        return scores
    parts = [
        scores[place * TILE : (place + 1) * TILE] + tiles[last - place] for place in range(last + 1)
    ]
    return jnp.concatenate(parts, 0) if len(parts) > 1 else parts[0]


def attend_block(q_ref, k_ref, v_t, o_ref, lse_ref, tiles_ref, start, last, span):
    query = q_ref[start : start + TILE, :]
    size = query.shape[1] // PAIR
    mixed = []
    for head in range(PAIR):
        tiles = None if tiles_ref is None else tiles_ref.at[head]
        scores = scores_t(k_ref[:span, :], keep_head(query, head), tiles, last)
        summit = jnp.max(scores, 0, keepdims=True)
        exponent = jnp.exp(scores - summit)
        total = jnp.sum(exponent, 0, keepdims=True)
        weighted = contract(
            v_t[head * size : (head + 1) * size, :span], exponent.astype(LOW), 1, 0
        )
        mixed.append(weighted / total)
        lse_ref[0, head : head + 1, start : start + TILE] = summit + jnp.log(total)
    o_ref[start : start + TILE, :] = jnp.concatenate(mixed, 0).T.astype(LOW)


def attend_kernel(causal, *refs):
    if causal:
        seq_ref, q_ref, k_ref, v_ref, z_ref, o_ref, lse_ref, tiles_ref = refs
        make_tiles(z_ref, tiles_ref)
    else:
        q_ref, k_ref, v_ref, o_ref, lse_ref = refs
    v_t = v_ref[...].T
    blocks = q_ref.shape[0] // TILE
    keys = k_ref.shape[0]
    if not causal:
        for block in range(blocks):
            attend_block(q_ref, k_ref, v_t, o_ref, lse_ref, None, block * TILE, None, keys)
        return
    for side in range(keys // q_ref.shape[0]):

        @pl.when(seq_ref[0] == side)
        def _(side=side):
            for block in range(blocks):
                last = side * blocks + block
                attend_block(
                    q_ref, k_ref, v_t, o_ref, lse_ref, tiles_ref, block * TILE, last,
                    (last + 1) * TILE,
                )


def make_tiles(z_ref, tiles_ref):
    for head in range(PAIR):
        for off in range(z_ref.shape[2]):
            tiles_ref[head, off] = toeplitz(z_ref[0, head, off : off + 1, :])


def attend(queries, keys_all, values, seq_pos, rows):
    count, width = queries.shape
    length = keys_all.shape[0]
    pairs = H // PAIR
    lanes = width // pairs
    offs = length // TILE
    causal = rows is not None
    col = lambda size: pl.BlockSpec((size, lanes), lambda pair, *_: (0, pair))
    in_specs = [col(count), col(length), col(length)]
    args = [queries, keys_all, values]
    scratch = []
    if causal:
        in_specs.append(pl.BlockSpec((1, PAIR, offs, 2 * TILE), lambda pair, *_: (pair, 0, 0, 0)))
        args = [seq_pos] + args + [rows]
        scratch = [pltpu.VMEM((PAIR, offs, TILE, TILE), F32)]
    work = H * count * length
    return pl.pallas_call(
        functools.partial(attend_kernel, causal),
        grid_spec=pltpu.PrefetchScalarGridSpec(
            num_scalar_prefetch=1 if causal else 0,
            grid=(pairs,),
            in_specs=in_specs,
            out_specs=[
                col(count),
                pl.BlockSpec((1, PAIR, count), lambda pair, *_: (pair, 0, 0)),
            ],
            scratch_shapes=scratch,
        ),
        out_shape=[
            jax.ShapeDtypeStruct((count, width), LOW),
            jax.ShapeDtypeStruct((pairs, PAIR, count), F32),
        ],
        cost_estimate=pl.CostEstimate(
            flops=work * 256 * 2, bytes_accessed=6 * length * width, transcendentals=work
        ),
        name="attend_causal" if causal else "attend_cross",
    )(*args)


def back_block(refs, k_t, prod_t, start, last, span, first, tiles_ref, total_ref):
    q_ref, k_ref, v_ref, g_ref, lse_ref, dq_ref, dk_acc, dv_acc = refs
    query = q_ref[start : start + TILE, :]
    grad = g_ref[start : start + TILE, :]
    size = query.shape[1] // PAIR
    dq_t = []
    dk = dv = None
    for head in range(PAIR):
        own = keep_head(query, head)
        own_grad = keep_head(grad, head)
        tiles = None if tiles_ref is None else tiles_ref.at[head]
        scores = scores_t(k_ref[:span, :], own, tiles, last)
        probs = jnp.exp(scores - lse_ref[0, head : head + 1, start : start + TILE])
        grad_probs = contract(v_ref[:span, :], own_grad, 1, 1)
        delta = jnp.sum(
            prod_t[head * size : (head + 1) * size, start : start + TILE], 0, keepdims=True
        )
        grad_scores = probs * (grad_probs - delta)
        low = grad_scores.astype(LOW)
        dv_new = contract(probs.astype(LOW), own_grad, 1, 0)
        dk_new = contract(low, own, 1, 0)
        dv = dv_new if dv is None else dv + dv_new
        dk = dk_new if dk is None else dk + dk_new
        dq_t.append(contract(k_t[head * size : (head + 1) * size, :span], low, 1, 0))
        if total_ref is not None:
            for place in range(last + 1):
                off = last - place
                piece = grad_scores[place * TILE : (place + 1) * TILE]
                if first:
                    total_ref[head, off] = piece
                elif off == last:
                    total_ref[head, off] = piece
                else:
                    total_ref[head, off] += piece
    dq_ref[start : start + TILE, :] = jnp.concatenate(dq_t, 0).T.astype(LOW)
    if first:
        dk_acc[:span, :] = dk
        dv_acc[:span, :] = dv
        if span < dk_acc.shape[0]:
            dk_acc[span:, :] = jnp.zeros((dk_acc.shape[0] - span, dk_acc.shape[1]), F32)
            dv_acc[span:, :] = jnp.zeros((dv_acc.shape[0] - span, dv_acc.shape[1]), F32)
    else:
        dk_acc[:span, :] += dk
        dv_acc[:span, :] += dv


def back_kernel(causal, *refs):
    if causal:
        (seq_ref, q_ref, k_ref, v_ref, g_ref, o_ref, lse_ref, z_ref,
         dq_ref, dk_ref, dv_ref, row_ref, dk_acc, dv_acc, tiles_ref, total_ref) = refs
        make_tiles(z_ref, tiles_ref)
    else:
        (q_ref, k_ref, v_ref, g_ref, o_ref, lse_ref,
         dq_ref, dk_ref, dv_ref, dk_acc, dv_acc) = refs
        tiles_ref = total_ref = None
    k_t = k_ref[...].T
    prod_t = (g_ref[...].astype(F32) * o_ref[...].astype(F32)).T
    blocks = q_ref.shape[0] // TILE
    keys = k_ref.shape[0]
    main = (q_ref, k_ref, v_ref, g_ref, lse_ref, dq_ref, dk_acc, dv_acc)
    if not causal:
        for block in range(blocks):
            back_block(main, k_t, prod_t, block * TILE, None, keys, block == 0, None, None)
    else:
        for side in range(keys // q_ref.shape[0]):

            @pl.when(seq_ref[0] == side)
            def _(side=side):
                for block in range(blocks):
                    last = side * blocks + block
                    back_block(
                        main, k_t, prod_t, block * TILE, last, (last + 1) * TILE,
                        block == 0, tiles_ref, total_ref,
                    )
                for head in range(PAIR):
                    for off in range(keys // TILE):
                        if off < (side + 1) * blocks:
                            row_ref[0, head, off : off + 1, :] = skew_sum(total_ref.at[head, off])
                        else:
                            row_ref[0, head, off : off + 1, :] = jnp.zeros((1, 2 * TILE), F32)

    dk_ref[...] = dk_acc[...].astype(LOW)
    dv_ref[...] = dv_acc[...].astype(LOW)


def attend_back(queries, keys_all, values, grad_mixed, mixed, lse, seq_pos, rows):
    count, width = queries.shape
    length = keys_all.shape[0]
    pairs = H // PAIR
    lanes = width // pairs
    offs = length // TILE
    causal = rows is not None
    col = lambda size: pl.BlockSpec((size, lanes), lambda pair, *_: (0, pair))
    in_specs = [col(count), col(length), col(length), col(count), col(count),
                pl.BlockSpec((1, PAIR, count), lambda pair, *_: (pair, 0, 0))]
    out_specs = [col(count), col(length), col(length)]
    out_shape = [
        jax.ShapeDtypeStruct((count, width), LOW),
        jax.ShapeDtypeStruct((length, width), LOW),
        jax.ShapeDtypeStruct((length, width), LOW),
    ]
    args = [queries, keys_all, values, grad_mixed, mixed, lse]
    scratch = [pltpu.VMEM((length, lanes), F32), pltpu.VMEM((length, lanes), F32)]
    if causal:
        row_spec = pl.BlockSpec((1, PAIR, offs, 2 * TILE), lambda pair, *_: (pair, 0, 0, 0))
        in_specs.append(row_spec)
        out_specs.append(row_spec)
        out_shape.append(jax.ShapeDtypeStruct((pairs, PAIR, offs, 2 * TILE), F32))
        args = [seq_pos] + args + [rows]
        scratch += [pltpu.VMEM((PAIR, offs, TILE, TILE), F32)] * 2
    work = H * count * length
    return pl.pallas_call(
        functools.partial(back_kernel, causal),
        grid_spec=pltpu.PrefetchScalarGridSpec(
            num_scalar_prefetch=1 if causal else 0,
            grid=(pairs,),
            in_specs=in_specs,
            out_specs=out_specs,
            scratch_shapes=scratch,
        ),
        out_shape=out_shape,
        cost_estimate=pl.CostEstimate(
            flops=work * 640 * 2, bytes_accessed=12 * length * width, transcendentals=work
        ),
        name="attend_causal_back" if causal else "attend_cross_back",
    )(*args)


def bucket_rows(buckets, length):
    offs = length // TILE
    place = jnp.arange(2 * TILE, dtype=jnp.int32)
    step = jnp.where(place < TILE, place, place - 2 * TILE)
    gap = (jnp.arange(offs, dtype=jnp.int32) * TILE)[:, None] + step[None, :]
    marks = jnp.arange(BUCKETS, dtype=jnp.int32)
    begins = jnp.sum((buckets[None, :] < marks[:, None]).astype(jnp.int32), 1)
    ends = jnp.sum((buckets[None, :] <= marks[:, None]).astype(jnp.int32), 1)
    hot = (gap[None] >= begins[:, None, None]) & (gap[None] < ends[:, None, None])
    return (gap, hot.astype(LOW))


def bit_plan():
    bits = []
    for axis in ("seq", "shard"):
        size = lax.axis_size(axis)
        assert size & (size - 1) == 0
        bits += [(axis, place) for place in reversed(range(size.bit_length() - 1))]
    return bits


def bit_orders(bits):
    ends = [0, len(bits) - 2, len(bits) - 1]
    rest = [place for place in range(len(bits)) if place not in ends]
    flipped = [ends[1], ends[0], ends[2]]
    return (rest + ends, rest + flipped, ends[:2] + rest + ends[2:])


def coords(bits):
    return [lax.rem(lax.axis_index(axis) // (1 << place), 2) for axis, place in bits]


def partner(bits, which):
    axis, place = bits[which]
    index = lax.axis_index(axis)
    mine = lax.rem(index // (1 << place), 2)
    return {axis: index + (1 - 2 * mine) * (1 << place)}


def greet(bits):
    barrier = pltpu.get_barrier_semaphore()
    for which in range(len(bits)):
        pl.semaphore_signal(
            barrier, inc=1, device_id=partner(bits, which), device_id_type=pl.DeviceIdType.MESH
        )
    pl.semaphore_wait(barrier, len(bits))


def remote(bits, which, source, target, sems):
    return pltpu.make_async_remote_copy(
        src_ref=source,
        dst_ref=target,
        send_sem=sems[0],
        recv_sem=sems[1],
        device_id=partner(bits, which),
        device_id_type=pl.DeviceIdType.MESH,
    )


def send(*args):
    copy = remote(*args)
    copy.start()
    return copy


def scatter_kernel(bits, count, *refs):
    steps = len(bits)
    sources, outs, work = refs[:count], refs[count : 2 * count], refs[2 * count : 3 * count]
    arrivals = refs[3 * count : (3 + steps) * count]
    load_sem, send_sem, recv_sem = refs[(3 + steps) * count :]
    place = coords(bits)
    orders = [list(reversed(order)) for order in bit_orders(bits)[:2]]
    loads = []
    for item in range(count):
        load = pltpu.make_async_copy(sources[item], work[item], load_sem.at[item])
        load.start()
        loads.append(load)
    greet(bits)
    copies = {}

    def add(item, step):
        order = orders[item % 2]
        free = [which for which in range(steps) if which not in order[: step + 1]]
        arrived = arrivals[item * steps + step]
        copies[item, step].wait_recv()
        if not free:
            outs[item][...] = work[item][tuple(place)].astype(F32) + arrived[...].astype(F32)
            return

        @pl.loop(0, 1 << len(free))
        def _(block):
            sub = [lax.rem(block // (1 << (len(free) - 1 - i)), 2) for i in range(len(free))]
            here = tuple(
                sub[free.index(which)] if which in free else place[which] for which in range(steps)
            )
            total = work[item][here].astype(F32) + arrived[tuple(sub)].astype(F32)
            work[item][here] = total.astype(work[item].dtype)

    for turn in range(steps + 1 + (count - 1) // 2):
        for item in range(count):
            step = turn - item // 2
            if not 0 <= step <= steps:
                continue
            if step == 0:
                loads[item].wait()
            else:
                add(item, step - 1)
            if step == steps:
                continue
            order = orders[item % 2]
            there = tuple(
                1 - place[which]
                if which == order[step]
                else (place[which] if which in order[:step] else slice(None))
                for which in range(steps)
            )
            copies[item, step] = send(
                bits,
                order[step],
                work[item].at[there],
                arrivals[item * steps + step],
                (send_sem.at[item, step], recv_sem.at[item, step]),
            )
    for copy in copies.values():
        copy.wait_send()


def scatter(items, collective_id):
    bits = bit_plan()
    steps = len(bits)
    count = len(items)
    sems = pltpu.SemaphoreType.DMA((count, steps))
    owners = 1 << steps
    items = [x.reshape((2,) * steps + (x.shape[0] // owners,) + x.shape[1:]) for x in items]
    tails = [x.shape[steps:] for x in items]
    arrivals = [
        pltpu.VMEM((2,) * (steps - 1 - step) + tail, x.dtype)
        for x, tail in zip(items, tails)
        for step in range(steps)
    ]
    return pl.pallas_call(
        functools.partial(scatter_kernel, bits, count),
        out_shape=[jax.ShapeDtypeStruct(tail, F32) for tail in tails],
        in_specs=[pl.BlockSpec(memory_space=pl.ANY)] * count,
        out_specs=[pl.BlockSpec(memory_space=pltpu.VMEM)] * count,
        scratch_shapes=[pltpu.VMEM(x.shape, x.dtype) for x in items]
        + arrivals
        + [pltpu.SemaphoreType.DMA((count,)), sems, sems],
        compiler_params=pltpu.CompilerParams(collective_id=collective_id, has_side_effects=True),
        name="scatter_rows",
    )(*items)


def table_rows(smalls, table_size, row):
    flat = smalls.reshape(-1, smalls.shape[-1])
    count = table_size * flat.shape[0] // 8
    entry = lax.broadcasted_iota(jnp.int32, (count, flat.shape[0]), 0)
    source = lax.broadcasted_iota(jnp.int32, (count, flat.shape[0]), 1)
    begin = (source >> 3) * table_size
    pick = ((source & 7) == row) & (entry >= begin) & (entry < begin + table_size)
    spread = contract(pick.astype(LOW), flat.astype(LOW), 1, 0)
    lane = lax.broadcasted_iota(jnp.int32, spread.shape, 1)
    place = lax.broadcasted_iota(jnp.int32, spread.shape, 0).astype(F32)
    block = jnp.floor((place + 0.5) * (1.0 / table_size))
    return jnp.where(lane.astype(F32) == place - block * table_size, spread, 0.0)


def gain_row(smalls, size, row):
    flat = smalls.reshape(-1, smalls.shape[-1])
    count = size * flat.shape[0] // 8
    source = lax.broadcasted_iota(jnp.int32, (flat.shape[0], count), 0)
    entry = lax.broadcasted_iota(jnp.int32, (flat.shape[0], count), 1)
    begin = (source >> 3) * size
    pick = ((source & 7) == row) & (entry >= begin) & (entry < begin + size)
    spread = contract(flat.astype(LOW), pick.astype(LOW), 0, 0)
    lane = lax.broadcasted_iota(jnp.int32, spread.shape, 0).astype(F32)
    place = lax.broadcasted_iota(jnp.int32, spread.shape, 1).astype(F32)
    block = jnp.floor((place + 0.5) * (1.0 / size))
    return jnp.sum(jnp.where(lane == place - block * size, spread, 0.0), 0, keepdims=True)


def full_weight(ref):
    value = ref[...].astype(F32)
    return value.reshape(-1, value.shape[-1]).astype(LOW)


ARRAYS = 12
INSIDE = 9
ITEMS = 15
PIECES = tuple((array, None, 0) for array in range(INSIDE)) + tuple(
    (array, axis, half) for array, axis in ((9, 1), (10, 1), (11, 0)) for half in range(2)
)
PATHS = ('xzZyc', 'xzZyc', 'zZxyc', 'zZyxc', 'yxzZc', 'xzZyc', 'zZxyc', 'zZxyc', 'xyzZc', 'zZyxc', 'zZyxc', 'xzZyc', 'yzZxc', 'xzZyc', 'xyzZc')
PLAN = (
    (1, 0, 0), (3, 0, 0), (2, 0, 0), (0, 0, 0), (14, 0, 0), (15, 0, 0),
    (1, 1, 0), (3, 1, 0), (0, 1, 0), (2, 1, 0), (7, 0, 0), (6, 0, 0),
    (1, 2, 0), (3, 2, 0), (9, 0, 0), (10, 0, 0), (11, 0, 0), (2, 2, 0),
    (7, 1, 0), (4, 0, 0), (0, 2, 0), (5, 0, 0), (12, 0, 0), (9, 1, 0),
    (1, 3, 0), (12, 1, 0), (10, 1, 0), (13, 0, 0), (6, 1, 0), (0, 3, 0),
    (8, 0, 0), (4, 1, 0), (11, 1, 0), (3, 3, 0), (14, 1, 0), (1, 4, 0),
    (2, 3, 0), (0, 4, 0), (5, 1, 0), (12, 2, 0), (6, 2, 0), (8, 1, 0),
    (4, 2, 0), (7, 2, 0), (5, 2, 1), (9, 2, 1), (11, 2, 1), (10, 2, 1),
    (13, 1, 1), (2, 4, 1), (14, 2, 2), (16, 0, 2), (12, 3, 2), (3, 4, 2),
    (6, 3, 3), (4, 3, 6), (5, 3, 6), (13, 2, 7), (8, 2, 7), (10, 3, 7),
    (6, 4, 7), (7, 3, 8), (11, 3, 8), (9, 3, 8), (14, 3, 8), (4, 4, 9),
    (5, 4, 9), (8, 3, 11), (13, 3, 11), (7, 4, 11), (12, 4, 14), (11, 4, 16),
    (14, 4, 17), (10, 4, 17), (8, 4, 18), (13, 4, 18), (9, 4, 19),
)
(STAGE_GAIN, STAGE_QUERY, STAGE_KEY, STAGE_VALUE, STAGE_SELF, STAGE_OUT, STAGE_CQUERY, STAGE_CKEY,
 STAGE_CVALUE, STAGE_CROSS, STAGE_COUT, STAGE_END) = (0, 1, 2, 3, 4, 10, 11, 12, 13, 14, 20, 21)


def path_bits(bits, path):
    count = len(bits)
    rest = list(range(1, count - 2))
    groups = {"x": [0], "y": [count - 2], "c": [count - 1], "z": rest[:-1], "Z": rest[-1:]}
    return [groups[letter] for letter in path]


def open_kernel(bits, sizes, *refs):
    gain_size, table_size = sizes
    sources = refs[:ARRAYS]
    hidden_ref, enc_ref, hot_ref, mask_ref = refs[ARRAYS : ARRAYS + 4]
    outs = refs[ARRAYS + 4 : 2 * ARRAYS + 4]
    (enc_out, first_out, q_out, k_out, v_out, mixed_out, lse_out, after_out, second_out,
     cq_out, ck_out, cv_out, cmixed_out, clse_out, across_out, third_out,
     before_ref, flat_ref, tiles_ref, weight_ref,
     send_sem, recv_sem, own_sem, side_send, side_recv) = refs[2 * ARRAYS + 4 :]
    steps = len(bits)
    place = coords(bits)
    seq_pos = lax.axis_index("seq")
    rows = hidden_ref.shape[0]
    keys = first_out.shape[0]
    lanes = hidden_ref.shape[1] // (H // PAIR)

    def own(array):
        return pltpu.make_async_copy(
            sources[array], outs[array].at[tuple(place)], own_sem.at[array]
        )

    def copy(item, step):
        order = sum(path_bits(bits, PATHS[item]), [])
        array, axis, half = PIECES[item]
        here = tuple(
            slice(None) if which in order[:step] else place[which] for which in range(steps)
        )
        part = ()
        if axis is not None:
            size = sources[array].shape[axis] // 2
            part = (slice(None),) * axis + (pl.ds(half * size, size),)
        target = outs[array].at[here + part]
        source = target
        if step == 0:
            source = sources[array].at[part] if part else sources[array]
        return remote(
            bits,
            order[step],
            source,
            target,
            (send_sem.at[item, step], recv_sem.at[item, step]),
        )

    def arrived(item):
        copy(item, steps - 1).wait_recv()

    def side(which):
        source, target = ((hidden_ref, before_ref), (enc_ref, enc_out.at[rows:]))[which]
        return remote(bits, 0, source, target, (side_send.at[which], side_recv.at[which]))

    todo = list(PLAN)
    seen = set()

    def advance(until):
        while todo and todo[0][2] <= until:
            item, step, _ = todo.pop(0)
            if item >= ITEMS:
                side(item - ITEMS).start()
                continue
            groups = path_bits(bits, PATHS[item])
            first = sum(len(group) for group in groups[:step])
            for number in range(first, first + len(groups[step])):
                if number > 0:
                    if PIECES[item][0] not in seen:
                        seen.add(PIECES[item][0])
                        own(PIECES[item][0]).wait()
                    copy(item, number - 1).wait_recv()
                copy(item, number).start()

    for array in range(ARRAYS):
        own(array).start()
    greet(bits)
    enc_out[:rows, :] = enc_ref[...]
    advance(STAGE_GAIN)
    arrived(0)
    gains = [gain_row(outs[0][...], gain_size, row) for row in range(3)]
    flat_ref[...] = table_rows(outs[0][...], table_size, 3)

    def normed(value, gain):
        scale = lax.rsqrt(jnp.mean(value * value, -1, keepdims=True) + EPSILON)
        return (value * scale * gain).astype(LOW)

    def over_rows(count, body):
        @pl.loop(0, count // TILE)
        def _(block):
            body(lambda base=0: pl.ds(base + pl.multiple_of(block * TILE, TILE), TILE))

    def normed_rows(source, start):
        def body(at):
            first_out[at(start), :] = normed(source[at(), :].astype(F32), gains[0])

        over_rows(rows, body)

    def project(item, source, out, begin, count):
        weight_ref[...] = full_weight(outs[item])

        def body(at):
            out[at(), :] = contract(source[at(begin), :], weight_ref[...], 1, 0).astype(LOW)

        over_rows(count, body)

    normed_rows(hidden_ref, rows)
    advance(STAGE_QUERY)
    arrived(1)
    project(1, first_out, q_out, rows, rows)
    advance(STAGE_KEY)
    side(0).wait_recv()

    @pl.when(seq_pos == 0)
    def _():
        first_out[:rows, :] = first_out[rows:, :]

    @pl.when(seq_pos != 0)
    def _():
        normed_rows(before_ref, 0)

    arrived(2)
    project(2, first_out, k_out, 0, keys)
    advance(STAGE_VALUE)
    arrived(3)
    project(3, first_out, v_out, 0, keys)

    advance(STAGE_SELF)

    def between(pair, begin):
        for done in range(H // PAIR - 1):

            @pl.when(pair == done)
            def _(done=done):
                advance(begin + done + 1)

    @pl.loop(0, H // PAIR)
    def _(pair):
        at = pl.ds(pl.multiple_of(pair * lanes, lanes), lanes)
        q_ref, k_ref, v_ref, o_ref = (ref.at[:, at] for ref in (q_out, k_out, v_out, mixed_out))
        for head in range(PAIR):
            column = jnp.sum(
                flat_ref[pl.ds(pl.multiple_of((pair * PAIR + head) * BUCKETS, BUCKETS), BUCKETS), :],
                1,
                keepdims=True,
            )
            for off in range(keys // TILE):
                row = jnp.sum(column * hot_ref[off].astype(F32), 0, keepdims=True)
                tiles_ref[head, off] = toeplitz(row + mask_ref[off])
        v_t = v_ref[...].T
        blocks = rows // TILE
        for part in range(keys // rows):

            @pl.when(seq_pos == part)
            def _(part=part):
                for block in range(blocks):
                    last = part * blocks + block
                    attend_block(
                        q_ref, k_ref, v_t, o_ref, lse_out.at[pl.ds(pair, 1)], tiles_ref,
                        block * TILE, last, (last + 1) * TILE,
                    )

        between(pair, STAGE_SELF)

    def residual(item, mixed, base, total, normal, gain):
        weight_ref[...] = full_weight(outs[item])

        def body(at):
            value = base[at(), :].astype(F32) + contract(mixed[at(), :], weight_ref[...], 1, 0)
            total[at(), :] = value
            normal[at(), :] = normed(value, gain)

        over_rows(rows, body)

    advance(STAGE_OUT)
    arrived(4)
    residual(4, mixed_out, hidden_ref, after_out, second_out, gains[1])
    advance(STAGE_CQUERY)
    arrived(5)
    project(5, second_out, cq_out, 0, rows)
    advance(STAGE_CKEY)
    side(1).wait_recv()
    arrived(6)
    project(6, enc_out, ck_out, 0, keys)
    advance(STAGE_CVALUE)
    arrived(7)
    project(7, enc_out, cv_out, 0, keys)
    advance(STAGE_CROSS)

    @pl.loop(0, H // PAIR)
    def _(pair):
        at = pl.ds(pl.multiple_of(pair * lanes, lanes), lanes)
        q_ref, k_ref, v_ref, o_ref = (ref.at[:, at] for ref in (cq_out, ck_out, cv_out, cmixed_out))
        v_t = v_ref[...].T
        for block in range(rows // TILE):
            attend_block(
                q_ref, k_ref, v_t, o_ref, clse_out.at[pl.ds(pair, 1)], None, block * TILE, None, keys
            )
        between(pair, STAGE_CROSS)

    advance(1000)

    arrived(8)
    residual(8, cmixed_out, after_out, across_out, third_out, gains[2])
    for item in range(INSIDE, ITEMS):
        arrived(item)
    for item in range(ITEMS):
        for step in range(steps):
            copy(item, step).wait_send()
    for which in range(2):
        side(which).wait_send()


def open_layer(items, hidden, encoded, hot, mask, sizes, collective_id):
    bits = bit_plan()
    steps = len(bits)
    count, width = hidden.shape
    length = count * lax.axis_size("seq")
    offs = length // TILE
    sems = pltpu.SemaphoreType.DMA((ITEMS, steps))
    inside = pl.BlockSpec(memory_space=pltpu.VMEM)
    outside = pl.BlockSpec(memory_space=pl.ANY)
    few, many = (count, width), (length, width)
    lse = (H // PAIR, PAIR, count)
    shapes = [((2,) * steps + x.shape, x.dtype) for x in items]
    shapes += [(many, LOW), (many, LOW), (few, LOW), (many, LOW), (many, LOW), (few, LOW)]
    shapes += [(lse, F32), (few, F32), (few, LOW), (few, LOW), (many, LOW), (many, LOW)]
    shapes += [(few, LOW), (lse, F32), (few, F32), (few, LOW)]
    outs = pl.pallas_call(
        functools.partial(open_kernel, bits, sizes),
        out_shape=[jax.ShapeDtypeStruct(*x) for x in shapes],
        in_specs=[inside] * (ARRAYS + 4),
        out_specs=[inside] * INSIDE + [outside] * (ARRAYS - INSIDE) + [inside] * 16,
        scratch_shapes=[
            pltpu.VMEM((count, width), LOW),
            pltpu.VMEM((H * BUCKETS, 128), F32),
            pltpu.VMEM((PAIR, offs, TILE, TILE), F32),
            pltpu.VMEM((width, width), LOW),
            sems,
            sems,
            pltpu.SemaphoreType.DMA((ARRAYS,)),
            pltpu.SemaphoreType.DMA((2,)),
            pltpu.SemaphoreType.DMA((2,)),
        ],
        compiler_params=pltpu.CompilerParams(
            collective_id=collective_id, has_side_effects=True, vmem_limit_bytes=66_000_000
        ),
        name="open_layer",
    )(*items, hidden, encoded, hot, mask)
    return [out.reshape((-1,) + x.shape[-2:]) for out, x in zip(outs, items)] + list(outs[ARRAYS:])


def reversed_bits(bits, path):
    return list(reversed(sum(path_bits(bits, path), [])))


def close_kernel(bits, sizes, *refs):
    gain_size, table_size = sizes
    (ff_refs, weights, cross_refs, self_refs, (smalls_ref, hot_ref, mask_ref, hidden_in),
     (layer_out, hidden_out, enc_out), outs, (small_out,)) = take(refs, (7, 8, 7, 6, 4, 3, 11, 1))
    rest = refs[47:]
    arrivals = rest[: CLOSE_ITEMS * len(bits)]
    (work_ref, ff_work, down_work, small_ref, q_buf, k_buf, pair_buf, rows_buf, grad_buf,
     res_buf, after_buf, weight_buf, enc_own, send_buf, recv_buf, dk_acc, dv_acc,
     tiles_ref, total_ref, rows_ref, flat_ref, gain_sums, send_sem, recv_sem, side_send, side_recv,
     fetch_sem) = rest[CLOSE_ITEMS * len(bits) :]
    steps = len(bits)
    place = coords(bits)
    seq_pos = lax.axis_index("seq")
    rows = res_buf.shape[0]
    keys = k_buf.shape[0]
    lanes = res_buf.shape[1] // (H // PAIR)
    v_buf, keys_in_buf = pair_buf.at[0], pair_buf.at[1]
    mixed_buf, query_in_buf = rows_buf.at[0], rows_buf.at[1]

    def pick(names, which, side):
        return tuple(side if name == which else slice(None) for name in names)

    def order_of(item):
        return reversed_bits(bits, CLOSE_PATHS[item])

    def part_of(item):
        if item not in (DOWN, DOWN + 1):
            return ()
        size = outs[2].shape[0] // 2
        return (pl.ds((item - DOWN) * size, size),)

    def base(item):
        if item == SMALL:
            return small_ref
        if item < DOWN:
            return ff_work.at[item % 4]
        return down_work if item < SQUARES else work_ref.at[item % SLOTS]

    def arrival(item, step):
        return arrivals[item * steps + step]

    def names_at(item, step):
        order = order_of(item)
        return [which for which in range(steps) if which not in order[:step]]

    def copy(item, step):
        which = order_of(item)[step]
        names = names_at(item, step)
        there = pick(names, which, 1 - place[which])
        if step == 0:
            source = base(item).at[there + part_of(item)]
        else:
            source = arrival(item, step - 1).at[there]
        return remote(
            bits, which, source, arrival(item, step), (send_sem.at[item, step], recv_sem.at[item, step])
        )

    def add(item, step):
        which = order_of(item)[step]
        names = names_at(item, step)
        free = [name for name in names if name != which]
        target = arrival(item, step)
        copy(item, step).wait_recv()

        def one(sub):
            here = tuple(place[which] if name == which else sub[free.index(name)] for name in names)
            if step > 0:
                mine = arrival(item, step - 1)[here]
            else:
                mine = base(item)[here + part_of(item)]
            return mine.astype(F32) + target[tuple(sub)].astype(F32)

        if not free:
            if item == SMALL:
                small_out[...] = one(())
            elif item < DOWN:
                size = outs[0].shape[1] // FF_BLOCKS
                outs[item % 2][:, item // 2 * size : (item // 2 + 1) * size] = one(())
            elif item < SQUARES:
                outs[2][part_of(item)] = one(())
            else:
                outs[item - SQUARES + 3][...] = one(())
            return

        @pl.loop(0, 1 << len(free))
        def _(index):
            sub = [lax.rem(index // (1 << (len(free) - 1 - i)), 2) for i in range(len(free))]
            target[tuple(sub)] = one(sub).astype(target.dtype)

    def side(which):
        return remote(
            bits, 0, send_buf.at[which], recv_buf.at[which], (side_send.at[which], side_recv.at[which])
        )

    slots = {entry[:2]: entry[2] for entry in CLOSE_PLAN}
    done_slots = set()
    drained = set()

    def act(item, step):
        if item == CLOSE_ITEMS:
            side(0).start()
            return
        if item > CLOSE_ITEMS:

            @pl.when(seq_pos != 0)
            def _():
                side(1).start()

            return
        groups = list(reversed(path_bits(bits, CLOSE_PATHS[item]))) + [[None]]
        first = sum(len(group) for group in groups[:step])
        for number in range(first, first + len(groups[step])):
            if number > 0:
                add(item, number - 1)
            if number < steps:
                copy(item, number).start()

    def advance(slot):
        assert slot not in done_slots
        done_slots.add(slot)
        for item, step, planned in CLOSE_PLAN:
            if planned == slot:
                act(item, step)

    def drain(item, slot):
        assert slots[item, 1] <= slot
        copy(item, 0).wait_send()
        drained.add((item, 0))

    def fetch(source, target, sem):
        return pltpu.make_async_copy(source, target, fetch_sem.at[sem])

    def weight(number):
        return fetch(weights[number], weight_buf.at[number % 2], number % 2)

    def over_rows(count, body):
        @pl.loop(0, count // TILE)
        def _(block):
            body(lambda start=0: pl.ds(start + pl.multiple_of(block * TILE, TILE), TILE))

    def weight_grad(item, left, right):
        if item - SLOTS >= SQUARES:
            drain(item - SLOTS, max(done_slots))
        owner_grad(work_ref.at[item % SLOTS], left, right)

    def owner_grad(target, left, right):
        half = left.shape[1] // 2

        @pl.loop(0, 2)
        def _(top):
            at = pl.ds(pl.multiple_of(top * half, half), half)
            value = contract(left[:, at], right[...], 0, 0)
            target[top] = value.reshape(target.shape[1:]).astype(LOW)

    def pairs_back(lse_ref, tiles, begin):
        @pl.loop(0, H // PAIR)
        def _(pair):
            at = pl.ds(pl.multiple_of(pair * lanes, lanes), lanes)
            q_ref, k_ref, v_ref, g_ref, o_ref = (
                ref.at[:, at] for ref in (q_buf, k_buf, v_buf, grad_buf, mixed_buf)
            )
            if tiles:
                for head in range(PAIR):
                    start = pl.multiple_of((pair * PAIR + head) * BUCKETS, BUCKETS)
                    column = jnp.sum(flat_ref[pl.ds(start, BUCKETS), :], 1, keepdims=True)
                    for off in range(keys // TILE):
                        row = jnp.sum(column * hot_ref[off].astype(F32), 0, keepdims=True)
                        tiles_ref[head, off] = toeplitz(row + mask_ref[off])
            k_t = k_ref[...].T
            prod_t = (g_ref[...].astype(F32) * o_ref[...].astype(F32)).T
            main = (q_ref, k_ref, v_ref, g_ref, lse_ref.at[pl.ds(pair, 1)], q_ref, dk_acc, dv_acc)
            blocks = rows // TILE
            if not tiles:
                for block in range(blocks):
                    back_block(main, k_t, prod_t, block * TILE, None, keys, block == 0, None, None)
            else:
                for part in range(keys // rows):

                    @pl.when(seq_pos == part)
                    def _(part=part):
                        for block in range(blocks):
                            last = part * blocks + block
                            back_block(
                                main, k_t, prod_t, block * TILE, last, (last + 1) * TILE,
                                block == 0, tiles_ref, total_ref,
                            )
                        for head in range(PAIR):
                            column = jnp.zeros((BUCKETS, 1), F32)
                            for off in range((part + 1) * blocks):
                                row = skew_sum(total_ref.at[head, off])
                                column = column + jnp.sum(
                                    hot_ref[off].astype(F32) * row, 1, keepdims=True
                                )
                            start = pl.multiple_of((pair * PAIR + head) * BUCKETS, BUCKETS)
                            rows_ref[pl.ds(start, BUCKETS), :] = jnp.broadcast_to(
                                column, (BUCKETS, rows_ref.shape[1])
                            )

            k_ref[...] = dk_acc[...].astype(LOW)
            v_ref[...] = dv_acc[...].astype(LOW)
            for done in range(H // PAIR - 1):

                @pl.when(pair == done)
                def _(done=done):
                    advance(begin + done + 1)

    cq_in, ck_in, cv_in, cmixed_in, enc_in, second_in, clse_ref = cross_refs
    q_in, k_in, v_in, mixed_in, first_in, lse_ref = self_refs[:6]
    fetches = [
        fetch(cmixed_in, mixed_buf, 2), fetch(cq_in, q_buf, 3), fetch(ck_in, k_buf, 4),
        fetch(cv_in, v_buf, 5), fetch(enc_in, keys_in_buf, 6), fetch(second_in, query_in_buf, 7),
    ]
    third_in, grad_in, across_in, gate_in, up_in, down_in, after_in = ff_refs
    width = gate_in.shape[1] // FF_BLOCKS
    third_ref, grad_ref = k_buf.at[:rows], k_buf.at[rows:]
    loads = [fetch(third_in, third_ref, 2), fetch(grad_in, grad_ref, 3), fetch(across_in, after_buf, 4)]

    def ff_loads(block, slot):
        at = pl.ds(pl.multiple_of(block * width, width), width)
        return (
            fetch(gate_in.at[:, at], weight_buf.at[slot, :, pl.ds(0, width)], 8 + slot),
            fetch(up_in.at[:, at], pair_buf.at[slot, pl.ds(0, weight_buf.shape[1]), pl.ds(0, width)],
                  10 + slot),
            fetch(down_in.at[at], rows_buf.at[slot, pl.ds(0, width)], 12 + slot),
        )

    for one in ff_loads(0, 0):
        one.start()
    for one in loads:
        one.start()
    greet(bits)
    flat_ref[...] = table_rows(smalls_ref[...], table_size, 3)
    gain_one, gain_two, gain_three = [gain_row(smalls_ref[...], gain_size, row) for row in range(3)]
    for one in loads:
        one.wait()
    res_buf[...] = jnp.zeros_like(res_buf)
    enc_own[...] = jnp.zeros_like(enc_own)

    def ff_rows(slot, at):
        w_gate = weight_buf[slot, :, 0:width]
        w_up = pair_buf[slot, 0 : weight_buf.shape[1], 0:width]
        w_down = rows_buf[slot, 0:width, :]
        gate = contract(third_ref[at, :], w_gate, 1, 0)
        upper = contract(third_ref[at, :], w_up, 1, 0)
        grad = contract(grad_ref[at, :], w_down, 1, 1)
        square = gate * gate
        bend = jnp.tanh(GELU_SCALE * gate * (1.0 + 0.044715 * square))
        open_part = 0.5 * (1.0 + bend)
        active = gate * open_part
        slope = open_part + 0.5 * gate * (1.0 - bend * bend) * (
            GELU_SCALE * (1.0 + 3.0 * 0.044715 * square)
        )
        inner = (active * upper).astype(LOW)
        gate_grad = (grad * upper * slope).astype(LOW)
        upper_grad = (grad * active).astype(LOW)
        q_buf[at, 0:width] = inner
        grad_buf[at, 0:width] = gate_grad
        send_buf[0, at, 0:width] = upper_grad
        res_buf[at, :] += contract(inner, w_down, 1, 0)
        enc_own[at, :] += contract(gate_grad, w_gate, 1, 1) + contract(upper_grad, w_up, 1, 1)

    @pl.loop(0, FF_BLOCKS)
    def _(block):
        slot = lax.rem(block, 2)
        for one in ff_loads(block, slot):
            one.wait()

        @pl.when(block < FF_BLOCKS - 1)
        def _():
            for one in ff_loads(block + 1, 1 - slot):
                one.start()

        @pl.loop(0, rows // TILE)
        def _(part):
            ff_rows(slot, pl.ds(pl.multiple_of(part * TILE, TILE), TILE))

        for now in range(FF_BLOCKS):

            @pl.when(block == now)
            def _(now=now):
                advance(2 + 2 * now)
                if now >= 2:
                    drain(2 * now - 4, 2 + 2 * now)
                    drain(2 * now - 3, 2 + 2 * now)

        owner_grad(ff_work.at[2 * slot], third_ref, grad_buf.at[:, 0:width])
        owner_grad(ff_work.at[2 * slot + 1], third_ref, send_buf.at[0, :, 0:width])
        value = contract(q_buf[:, 0:width], grad_ref[...], 0, 0)
        down_work[lax.div(block, 2), slot] = value.reshape(down_work.shape[2:]).astype(LOW)
        for now in range(FF_BLOCKS):

            @pl.when(block == now)
            def _(now=now):
                advance(3 + 2 * now)

    weight(0).start()
    weight(1).start()
    for one in (fetches[0], fetches[1], fetches[3], fetches[4], fetches[5]):
        one.start()

    def norm_back_rows(value, gain, grad):
        scale = lax.rsqrt(jnp.mean(value * value, -1, keepdims=True) + EPSILON)
        scaled = gain * grad
        inner = jnp.mean(value * scaled, -1, keepdims=True)
        back = scale * scaled - value * (scale * scale * scale) * inner
        return back, jnp.sum(grad * value * scale, 0, keepdims=True)

    gain_sums[...] = jnp.zeros_like(gain_sums)

    def body(at):
        value = after_buf[at(), :]
        send_buf[1, at(), :] = (value + res_buf[at(), :]).astype(LOW)
        back, total = norm_back_rows(value, gain_three, enc_own[at(), :])
        gain_sums[2:3, :] += total
        res_buf[at(), :] = grad_ref[at(), :].astype(F32) + back

    over_rows(rows, body)
    layer_copy = fetch(send_buf.at[1], layer_out, 15)
    layer_copy.start()
    fetch(after_in, after_buf, 14).start()
    fetches[2].start()

    def to_mixed(number, source):
        weight(number).wait()

        def body(at):
            grad_buf[at(), :] = contract(
                source[at(), :].astype(LOW), weight_buf[number % 2], 1, 1
            ).astype(LOW)

        over_rows(rows, body)
        weight(number + 2).start()

    advance(10)
    to_mixed(0, res_buf)
    fetches[0].wait()

    def low_rows(source, target):
        def body(at):
            target[at(), :] = source[at(), :].astype(LOW)

        over_rows(rows, body)

    low_rows(res_buf, send_buf.at[0])
    weight_grad(SQUARES, mixed_buf, send_buf.at[0])
    advance(11)
    for one in fetches[1:4]:
        one.wait()
    pairs_back(clse_ref, False, 11)
    fetch(mixed_in, mixed_buf, 2).start()
    advance(17)

    def both_back(numbers, keep, count):
        def body_other(at):
            total = contract(k_buf[at(count), :], weight_buf[numbers[0] % 2], 1, 1)
            total = total + contract(v_buf[at(count), :], weight_buf[numbers[1] % 2], 1, 1)
            send_buf[keep[0], at(), :] = total.astype(LOW)
            if not count:
                gain_sums[3:4, :] += jnp.sum(
                    total * keys_in_buf[at(), :].astype(F32), 0, keepdims=True
                )

        def body_own(at):
            begin = 0 if count else rows
            total = contract(k_buf[at(begin), :], weight_buf[numbers[0] % 2], 1, 1)
            total = total + contract(v_buf[at(begin), :], weight_buf[numbers[1] % 2], 1, 1)
            keep[1][at(), :] = total

        over_rows(rows, body_other)
        return body_own

    weight(1).wait()
    weight(2).wait()
    own_part = both_back((1, 2), (0, enc_own), rows)
    for one in fetches[4:]:
        one.wait()
    advance(18)
    weight_grad(SQUARES + 1, keys_in_buf, k_buf)
    advance(19)
    weight_grad(SQUARES + 2, keys_in_buf, v_buf)
    advance(20)
    over_rows(rows, own_part)
    fetch(k_in, k_buf, 4).start()
    fetch(v_in, v_buf, 5).start()
    fetch(first_in, keys_in_buf, 6).start()
    weight(3).start()
    weight(4).start()
    advance(21)
    weight_grad(SQUARES + 3, query_in_buf, q_buf)
    advance(22)
    weight(3).wait()
    fetch(after_in, after_buf, 14).wait()

    def body(at):
        grad = contract(q_buf[at(), :], weight_buf[1], 1, 1)
        back, total = norm_back_rows(after_buf[at(), :], gain_two, grad)
        gain_sums[1:2, :] += total
        res_buf[at(), :] += back

    over_rows(rows, body)
    fetch(q_in, q_buf, 3).start()
    weight(5).start()
    weight(4).wait()

    def body(at):
        grad_buf[at(), :] = contract(res_buf[at(), :].astype(LOW), weight_buf[0], 1, 1).astype(LOW)

    over_rows(rows, body)
    weight(6).start()
    fetch(mixed_in, mixed_buf, 2).wait()
    low_rows(res_buf, query_in_buf)
    weight_grad(SQUARES + 4, mixed_buf, query_in_buf)
    advance(23)
    fetch(q_in, q_buf, 3).wait()
    fetch(k_in, k_buf, 4).wait()
    fetch(v_in, v_buf, 5).wait()
    pairs_back(lse_ref, True, 23)
    advance(29)
    side(0).wait_recv()
    side(0).wait_send()

    def body(at):
        send_buf[0, at(), :] = (enc_own[at(), :] + recv_buf[0, at(), :].astype(F32)).astype(LOW)

    over_rows(rows, body)
    enc_copy = fetch(send_buf.at[0], enc_out, 8)
    enc_copy.start()
    fetch(hidden_in, grad_buf, 9).start()
    layer_copy.wait()
    weight(5).wait()
    weight(6).wait()
    fetch(first_in, keys_in_buf, 6).wait()
    own_part = both_back((5, 6), (1, enc_own), 0)

    advance(30)
    weight_grad(SQUARES + 5, keys_in_buf, v_buf)
    advance(31)
    weight_grad(SQUARES + 6, keys_in_buf, k_buf)
    advance(32)
    weight_grad(SQUARES + 7, keys_in_buf.at[rows:], q_buf)
    advance(33)
    over_rows(rows, own_part)
    weight(7).start()
    own_low = (seq_pos == 0).astype(F32)
    fetch(hidden_in, grad_buf, 9).wait()
    weight(7).wait()

    def body(at):
        grad = contract(q_buf[at(), :], weight_buf[1], 1, 1) + enc_own[at(), :]
        grad = grad + own_low * send_buf[1, at(), :].astype(F32)
        enc_own[at(), :] = grad
        value = grad_buf[at(), :].astype(F32)
        scale = lax.rsqrt(jnp.mean(value * value, -1, keepdims=True) + EPSILON)
        gain_sums[0:1, :] += jnp.sum(grad * value * scale, 0, keepdims=True)

    over_rows(rows, body)
    gain_sums[0:1, :] += (1.0 - own_low) * gain_sums[3:4, :] / gain_one
    small_ref[...] = small_rows(
        gain_sums[0:1, :], gain_sums[1:2, :], gain_sums[2:3, :], rows_ref[...], gain_size,
        table_size, small_ref.shape
    )
    advance(34)

    @pl.when(seq_pos == 0)
    def _():
        side(1).wait_recv()

    @pl.when(seq_pos != 0)
    def _():
        side(1).wait_send()

    def body(at):
        grad = enc_own[at(), :] + jnp.where(
            seq_pos == 0, recv_buf[1, at(), :].astype(F32), 0.0
        )
        back, _ = norm_back_rows(grad_buf[at(), :].astype(F32), gain_one, grad)
        hidden_out[at(), :] = (res_buf[at(), :] + back).astype(LOW)

    over_rows(rows, body)
    advance(35)
    assert all(entry[2] in done_slots for entry in CLOSE_PLAN)
    for item in range(CLOSE_ITEMS):
        for step in range(steps):
            if (item, step) not in drained:
                copy(item, step).wait_send()
    enc_copy.wait()


def take(refs, counts):
    out = []
    begin = 0
    for count in counts:
        out.append(refs[begin : begin + count])
        begin += count
    return out


def small_rows(one, two, three, table, gain_size, table_size, shape):
    owners = one.shape[1] // gain_size

    def spread(source, size, row):
        count = owners * size
        target = lax.broadcasted_iota(jnp.int32, (owners * 8, count), 0)
        entry = lax.broadcasted_iota(jnp.int32, (owners * 8, count), 1)
        begin = (target >> 3) * size
        hot = ((target & 7) == row) & (entry >= begin) & (entry < begin + size)
        return lax.dot_general(
            hot.astype(F32), source, (((1,), (0 if row == 3 else 1,)), ((), ())),
            precision=lax.Precision.HIGHEST, preferred_element_type=F32,
        )

    def wheel(shape, axis, size):
        entry = lax.broadcasted_iota(jnp.int32, shape, axis).astype(F32)
        lane = lax.broadcasted_iota(jnp.int32, shape, 1 - axis).astype(F32)
        return lane == entry - size * jnp.floor((entry + 0.5) * (1.0 / size))

    total = jnp.zeros((owners * 8, 128), F32)
    for row, value in enumerate((one, two, three)):
        grid = (128, value.shape[1])
        total = total + spread(
            jnp.where(wheel(grid, 1, gain_size), jnp.broadcast_to(value, grid), 0.0), gain_size, row
        )
    total = total + spread(jnp.where(wheel(table.shape, 0, table_size), table, 0.0), table_size, 3)
    return total.reshape(shape)


SLOTS = 2
FF_BLOCKS = 4
DOWN = 2 * FF_BLOCKS
SQUARES = DOWN + 2
SMALL = SQUARES + 8
CLOSE_ITEMS = SMALL + 1
GELU_SCALE = 0.7978845608028654
CLOSE_PATHS = ('xzZyc', 'xyzZc', 'yzZxc', 'yxzZc', 'xzZyc', 'yzZxc', 'xzZyc', 'yxzZc', 'yzZxc', 'xzZyc', 'zZyxc', 'xyzZc', 'xzZyc', 'xzZyc', 'zZyxc', 'zZxyc', 'xyzZc', 'zZxyc', 'xyzZc')
CLOSE_PLAN = (
    (1, 0, 3), (0, 0, 3), (0, 1, 4), (1, 1, 5), (3, 0, 5), (2, 0, 5),
    (3, 1, 6), (2, 1, 6), (1, 2, 9), (6, 0, 9), (9, 0, 9), (7, 0, 9),
    (8, 0, 10), (5, 0, 10), (0, 2, 11), (9, 1, 11), (6, 1, 11), (10, 0, 11),
    (4, 0, 12), (8, 1, 12), (7, 1, 12), (3, 2, 13), (2, 2, 13), (10, 1, 15),
    (9, 2, 15), (5, 1, 16), (19, 0, 19), (11, 0, 19), (8, 2, 19), (6, 2, 19),
    (4, 1, 20), (10, 2, 20), (12, 0, 20), (3, 3, 20), (11, 1, 21), (7, 2, 21),
    (0, 3, 22), (9, 3, 22), (12, 1, 22), (5, 2, 23), (14, 0, 23), (8, 3, 24),
    (13, 0, 24), (14, 1, 26), (7, 3, 26), (10, 3, 27), (12, 2, 27), (13, 1, 27),
    (4, 2, 27), (11, 2, 27), (6, 3, 27), (20, 0, 30), (14, 2, 30), (2, 3, 31),
    (15, 0, 31), (7, 4, 31), (13, 2, 31), (16, 0, 32), (1, 3, 32), (15, 1, 32),
    (5, 3, 32), (17, 0, 33), (16, 1, 33), (4, 3, 33), (12, 3, 33), (13, 3, 33),
    (17, 1, 33), (10, 4, 33), (11, 3, 34), (7, 5, 34), (18, 0, 34), (8, 4, 34),
    (15, 2, 34), (18, 1, 34), (16, 2, 34), (17, 2, 34), (1, 4, 34), (12, 4, 34),
    (2, 4, 34), (14, 3, 34), (15, 3, 34), (5, 4, 34), (11, 4, 34), (6, 4, 34),
    (18, 2, 34), (3, 4, 34), (9, 4, 34), (8, 5, 34), (17, 3, 34), (14, 4, 34),
    (16, 3, 34), (2, 5, 34), (5, 5, 34), (3, 5, 34), (0, 4, 34), (15, 4, 34),
    (10, 5, 34), (11, 5, 34), (18, 3, 34), (13, 4, 34), (1, 5, 34), (17, 4, 34),
    (4, 4, 34), (6, 5, 34), (9, 5, 34), (16, 4, 34), (18, 4, 34), (13, 5, 35),
    (4, 5, 35), (12, 5, 35), (14, 5, 35), (15, 5, 35), (18, 5, 35), (16, 5, 35),
    (0, 5, 35), (17, 5, 35),
)


def close_layer(forward, weights, cross, own, smalls, hot, mask, hidden, sizes, collective_id):
    bits = bit_plan()
    steps = len(bits)
    owners = 1 << steps
    count, width = hidden.shape
    units = forward[3].shape[1]
    length = cross[1].shape[0]
    offs = length // TILE
    lanes = width // (H // PAIR)
    gate, down = (width // owners, units), (units // owners, width)
    square = (width // owners, width)
    blocks = [(gate[0], units // FF_BLOCKS)] * DOWN + [(down[0] // 2, width)] * 2 + [square] * 8
    kinds = [LOW] * SMALL + [F32]
    blocks.append((8, 128))
    arrivals = [
        pltpu.VMEM((2,) * (steps - 1 - step) + block, kind)
        for block, kind in zip(blocks, kinds)
        for step in range(steps)
    ]
    inside = pl.BlockSpec(memory_space=pltpu.VMEM)
    outside = pl.BlockSpec(memory_space=pl.ANY)
    few, many = (count, width), (length, width)
    vm = pltpu.VMEM
    sems = pltpu.SemaphoreType.DMA((CLOSE_ITEMS, steps))
    pair_sem = pltpu.SemaphoreType.DMA((2,))
    return pl.pallas_call(
        functools.partial(close_kernel, bits, sizes),
        out_shape=[jax.ShapeDtypeStruct(few, LOW)] * 3
        + [jax.ShapeDtypeStruct(block, F32) for block in (gate, gate, down)]
        + [jax.ShapeDtypeStruct(square, F32)] * 8
        + [jax.ShapeDtypeStruct((8, 128), F32)],
        in_specs=[outside] * (7 + 8) + [outside] * 6 + [inside] + [outside] * 5 + [inside]
        + [inside] * 3 + [outside],
        out_specs=[outside, inside, outside] + [inside] * 12,
        scratch_shapes=arrivals
        + [
            vm((SLOTS,) + (2,) * steps + square, LOW),
            vm((4,) + (2,) * steps + (gate[0], units // FF_BLOCKS), LOW),
            vm((2,) * steps + down, LOW),
            vm((2,) * steps + (8, 128), F32),
            vm(few, LOW), vm(many, LOW), vm((2,) + many, LOW), vm((2,) + few, LOW),
            vm(few, LOW), vm(few, F32), vm(few, F32),
            vm((2, width, width), LOW), vm(few, F32), vm((2,) + few, LOW), vm((2,) + few, LOW),
            vm((length, lanes), F32), vm((length, lanes), F32),
            vm((PAIR, offs, TILE, TILE), F32), vm((PAIR, offs, TILE, TILE), F32),
            vm((H * BUCKETS, 128), F32), vm((H * BUCKETS, 128), F32), vm((8, width), F32),
            sems, sems, pair_sem, pair_sem, pltpu.SemaphoreType.DMA((16,)),
        ],
        compiler_params=pltpu.CompilerParams(
            collective_id=collective_id, has_side_effects=True, vmem_limit_bytes=67_000_000
        ),
        name="close_layer",
    )(*forward, *weights, *cross, *own, smalls, hot, mask, hidden)


def finish_kernel(*refs):
    count = (len(refs) - 5) // 2
    for source, target in zip(refs[: count], refs[count + 1 :]):
        target[...] = source[...]
    small = refs[count]
    for row, target in enumerate(refs[2 * count + 1 :]):
        target[...] = small[row, : target.shape[0]]


def finish(arrays, small, sizes):
    count = len(arrays)
    inside = pl.BlockSpec(memory_space=pltpu.VMEM)
    return pl.pallas_call(
        finish_kernel,
        out_shape=[jax.ShapeDtypeStruct(x.shape, x.dtype) for x in arrays]
        + [jax.ShapeDtypeStruct((size,), F32) for size in sizes],
        in_specs=[inside] * (count + 1),
        out_specs=[inside] * (count + 4),
        name="finish",
    )(*arrays, small)


def dot_low(left, right):
    return contract(left, right, 1, 0)


def dot_left(left, right):
    return contract(left, right, 0, 0)


def dot_right(left, right):
    return contract(left, right, 1, 1)


def rms_norm(value, gain):
    return value * lax.rsqrt(jnp.mean(value * value, -1, keepdims=True) + EPSILON) * gain


def norm_back(value, gain, grad):
    return jax.vjp(rms_norm, value, gain)[1](grad)


def gated(gate, upper):
    return jax.nn.gelu(gate, approximate=True) * upper


def pad_rows(rows, dtype):
    return jnp.stack([jnp.pad(row.astype(dtype), (0, 128 - row.shape[0])) for row in rows] + [
        jnp.zeros((128,), dtype)
    ] * (8 - len(rows)))


def on_device(
    hidden_in,
    encoded,
    cotangent,
    buckets,
    self_query,
    self_key,
    self_value,
    self_out,
    cross_query,
    cross_key,
    cross_value,
    cross_out,
    ff_gate,
    ff_up,
    ff_down,
    norm_self,
    norm_cross,
    norm_ff,
    bias_table,
):
    owners = lax.axis_size("seq") * lax.axis_size("shard")
    seq_pos = lax.axis_index("seq")
    seq_row = seq_pos.reshape(1).astype(jnp.int32)
    low_side = seq_pos == 0
    both = ("seq", "shard")
    width = hidden_in.shape[2]
    own_low = hidden_in[0]
    enc_own = encoded[0]
    small = pad_rows([norm_self, norm_cross, norm_ff, bias_table], F32)
    hidden = own_low.astype(F32)
    count = hidden.shape[0]
    length = count * lax.axis_size("seq")
    gap, hot = bucket_rows(buckets, length)
    hot_rows = jnp.swapaxes(hot, 0, 1)
    hot_mask = jnp.where(gap >= 0, 0.0, NEGATIVE)[:, None, :]
    opened = open_layer(
        [small, self_query, self_key, self_value, self_out, cross_query, cross_key, cross_value,
         cross_out, ff_gate, ff_up, ff_down],
        own_low,
        enc_own,
        hot_rows,
        hot_mask,
        (norm_self.shape[0], bias_table.shape[0]),
        1,
    )
    smalls = opened[0]
    (w_query, w_key, w_value, w_sout, w_cquery, w_ckey, w_cvalue, w_cout, w_gate, w_up, w_down) = [
        x.reshape(-1, x.shape[-1]) for x in opened[1:12]
    ]
    (enc_all, first_all, query, key, value, self_mixed, self_lse, after_self, second,
     cross_q, cross_k, cross_v, cross_mixed, cross_lse, after_cross, third) = opened[12:]
    gain_one, gain_two, gain_three = [
        smalls[:, i, : norm_self.shape[0]].reshape(-1) for i in range(3)
    ]
    table = smalls[:, 3, : bias_table.shape[0]].reshape(H, BUCKETS)
    rows = jnp.einsum("hb,bof->hof", table.astype(LOW), hot, preferred_element_type=F32)
    rows = jnp.where(gap[None] >= 0, rows, NEGATIVE).reshape(H // PAIR, PAIR, *gap.shape)
    first = first_all[count:]

    gains = norm_self.shape[0]
    if width // owners >= 16:
        *arrays, small_sum = close_layer(
            [third, cotangent[0], after_cross, w_gate, w_up, w_down, after_self],
            [w_cout, w_ckey, w_cvalue, w_cquery, w_sout, w_key, w_value, w_query],
            [cross_q, cross_k, cross_v, cross_mixed, enc_all, second, cross_lse],
            [query, key, value, self_mixed, first_all, self_lse],
            smalls,
            hot_rows,
            hot_mask,
            own_low,
            (gains, bias_table.shape[0]),
            2,
        )
        *arrays, one, two, three, four = finish(
            arrays, small_sum, (gains,) * 3 + bias_table.shape
        )
        hidden_out, grad_hidden, grad_encoded, *sums = arrays
        return (
            hidden_out[None],
            grad_hidden[None],
            grad_encoded[None],
            sums[10],
            sums[9],
            sums[8],
            sums[7],
            sums[6],
            sums[4],
            sums[5],
            sums[3],
            sums[0],
            sums[1],
            sums[2],
            one,
            two,
            three,
            four,
        )
    gate = dot_low(third, w_gate)
    upper = dot_low(third, w_up)
    inner = gated(gate, upper).astype(LOW)
    hidden_out = (after_cross + dot_low(inner, w_down)).astype(LOW)

    grad_top = cotangent[0]
    grad_wdown = dot_left(inner, grad_top).astype(LOW)
    grad_inner = dot_right(grad_top, w_down)
    grad_gate, grad_upper = jax.vjp(gated, gate, upper)[1](grad_inner)
    gate_low = grad_gate.astype(LOW)
    upper_low = grad_upper.astype(LOW)
    grad_wgate = dot_left(third, gate_low).astype(LOW)
    grad_wup = dot_left(third, upper_low).astype(LOW)
    grad_third = dot_right(gate_low, w_gate) + dot_right(upper_low, w_up)
    norm_grad, grad_gain_three = norm_back(after_cross, gain_three, grad_third)
    grad_cross_res = grad_top.astype(F32) + norm_grad
    sum_gate, sum_up = [
        lax.psum_scatter(x, both, scatter_dimension=0, tiled=True).astype(F32)
        for x in (grad_wgate, grad_wup)
    ]
    cross_res_low = grad_cross_res.astype(LOW)
    grad_wcout = dot_left(cross_mixed, cross_res_low).astype(LOW)
    grad_cross_mix = dot_right(cross_res_low, w_cout).astype(LOW)
    grad_cq, grad_ck, grad_cv = attend_back(
        cross_q, cross_k, cross_v, grad_cross_mix, cross_mixed, cross_lse, None, None
    )
    grad_enc = dot_right(grad_ck, w_ckey) + dot_right(grad_cv, w_cvalue)
    enc_back = lax.ppermute(grad_enc[count:].astype(LOW), "seq", [(0, 1), (1, 0)])
    grad_wcquery = dot_left(second, grad_cq).astype(LOW)
    grad_wckey = dot_left(enc_all, grad_ck).astype(LOW)
    grad_wcvalue = dot_left(enc_all, grad_cv).astype(LOW)
    norm_grad, grad_gain_two = norm_back(after_self, gain_two, dot_right(grad_cq, w_cquery))
    grad_self_res = grad_cross_res + norm_grad
    self_res_low = grad_self_res.astype(LOW)
    grad_wsout = dot_left(self_mixed, self_res_low).astype(LOW)
    grad_self_mix = dot_right(self_res_low, w_sout).astype(LOW)
    grad_q, grad_k, grad_v, grad_rows = attend_back(
        query, key, value, grad_self_mix, self_mixed, self_lse, seq_row, rows
    )
    grad_part = dot_right(grad_k, w_key) + dot_right(grad_v, w_value)
    part_back = lax.ppermute(grad_part[:count].astype(LOW), "seq", [(1, 0)])
    grad_wquery = dot_left(first, grad_q).astype(LOW)
    grad_wkey = dot_left(first_all, grad_k).astype(LOW)
    grad_wvalue = dot_left(first_all, grad_v).astype(LOW)
    grad_first = (
        dot_right(grad_q, w_query)
        + grad_part[count:]
        + jnp.where(low_side, grad_part[:count], 0.0)
        + part_back.astype(F32)
    )
    norm_grad, grad_gain_one = norm_back(hidden, gain_one, grad_first)
    grad_hidden = (grad_self_res + norm_grad).astype(LOW)
    grad_encoded = (grad_enc[:count] + enc_back.astype(F32)).astype(LOW)
    table_grad = jnp.einsum(
        "hof,bof->hb", grad_rows.reshape(H, *gap.shape), hot.astype(F32),
        precision=lax.Precision.HIGHEST,
    )
    small_grads = jnp.stack(
        [
            jnp.pad(x.reshape(owners, -1), ((0, 0), (0, 128 - x.size // owners)))
            for x in (grad_gain_one, grad_gain_two, grad_gain_three, table_grad)
        ]
        + [jnp.zeros((owners, 128), F32)] * 4,
        1,
    ).reshape(owners * 8, 128)
    sums = scatter(
        [grad_wdown, grad_wcout, grad_wcquery, grad_wckey, grad_wcvalue, grad_wsout, grad_wquery,
         grad_wkey, grad_wvalue, small_grads],
        2,
    )
    small_sum = sums[9]
    return (
        hidden_out[None],
        grad_hidden[None],
        grad_encoded[None],
        sums[6],
        sums[7],
        sums[8],
        sums[5],
        sums[2],
        sums[3],
        sums[4],
        sums[1],
        sum_gate,
        sum_up,
        sums[0],
        small_sum[0, :gains],
        small_sum[1, :gains],
        small_sum[2, :gains],
        small_sum[3, : bias_table.shape[0]],
    )


def solution(mesh):
    rows = P(("seq", "shard"), None)
    flat = P(("seq", "shard"))
    tokens = P("shard", "seq", None)
    return jax.shard_map(
        on_device,
        mesh=mesh,
        in_specs=(tokens,) * 3 + (P(),) + (rows,) * 11 + (flat,) * 4,
        out_specs=(tokens,) * 3 + (rows,) * 11 + (flat,) * 4,
        check_vma=False,
    )
```

profile of v0, /device:TPU:0, one launch (start us, length us, event | category | flops | bytes accessed | tf_op | source)
XLA Modules:
  0.0 254.6 jit_solution(5534482082524185963)
XLA Ops:
  0.7 0.8 convert_reduce_fusion.1
  1.5 0.7 bitcast_convert_fusion.2
  2.2 0.7 bitcast_convert_fusion
  2.9 0.6 stack.39.refs_0_
  3.5 0.7 compare_select_fusion.refs_15_.refs_30_
  4.1 0.1 broadcast_add_fusion
  4.2 0.8 and_convert_fusion.refs_14_.refs_29_
  5.0 107.4 %open_layer.1 = (f32[2,2,2,2,2,8,128]{6,5,4,3,2,1,0:T(8,128)}, bf16[2,2,2,2,2,24,768]{6,5,4,3,2,1,0:T(8,128)(2,1)}, bf16[2,2,2,2,2,24,768]{6,5,4,3,2,1,0:T(8,128...) custom-call(f32[8,128]{1,0:T(8,128)} %stack.39.refs_0_, ...), custom_call_target="tpu_custom_call" | custom-call | tf_op jit(solution)/shard_map/open_layer/pallas_call | solution.py:719
  112.3 138.0 %close_layer.1 = (bf16[512,768]{1,0:T(8,128)(2,1)}, bf16[512,768]{1,0:T(8,128)(2,1)}, bf16[512,768]{1,0:T(8,128)(2,1)}, f32[24,2048]{1,0:T(8,128)}, f32[24,2048]...) custom-call(bf16[512,768]{1,0:T(8,128)(2,1)} %get-tuple-element.79.r, ...), custom_call_target="tpu_custom_call" | custom-call | tf_op jit(solution)/shard_map/close_layer/pallas_call | solution.py:1330
  250.3 3.8 %finish.1 = (bf16[512,768]{1,0:T(8,128)(2,1)}, bf16[512,768]{1,0:T(8,128)(2,1)}, bf16[512,768]{1,0:T(8,128)(2,1)}, f32[24,2048]{1,0:T(8,128)}, f32[24,2048]{1,0:...) custom-call(bf16[512,768]{1,0:T(8,128)(2,1)} %get-tuple-element.107., ...), custom_call_target="tpu_custom_call" | custom-call | tf_op jit(solution)/shard_map/finish/pallas_call | solution.py:1372
  (3 shorter events, 0.0 us)
where the time goes:
time: 257 us; the launch traced here: 255 us
  Pallas kernels  249 us (97%)
  other arithmetic  3.69 us (1%)
    pallas_call x1, Pallas kernels, close_layer(): pl.pallas_call(functools.partial(close_kernel, bits, sizes), out_shape=[j...  138 us
    pallas_call x1, Pallas kernels, open_layer(): pl.pallas_call(functools.partial(open_kernel, bits, sizes), out_shape=[ja...  107 us

commit v1 on v0

--- a/solution.py
+++ b/solution.py
@@ -496,18 +496,31 @@
 def open_kernel(bits, sizes, *refs):
     gain_size, table_size = sizes
     sources = refs[:ARRAYS]
-    hidden_ref, enc_ref, hot_ref, mask_ref = refs[ARRAYS : ARRAYS + 4]
-    outs = refs[ARRAYS + 4 : 2 * ARRAYS + 4]
+    hidden_ref, enc_ref, buckets_ref = refs[ARRAYS : ARRAYS + 3]
+    finals = refs[ARRAYS + 3 : 2 * ARRAYS + 19]
+    kept = refs[2 * ARRAYS + 19 : 2 * ARRAYS + 35 + INSIDE]
+    outs = kept[:INSIDE] + finals[INSIDE:ARRAYS]
     (enc_out, first_out, q_out, k_out, v_out, mixed_out, lse_out, after_out, second_out,
-     cq_out, ck_out, cv_out, cmixed_out, clse_out, across_out, third_out,
-     before_ref, flat_ref, tiles_ref, weight_ref,
-     send_sem, recv_sem, own_sem, side_send, side_recv) = refs[2 * ARRAYS + 4 :]
+     cq_out, ck_out, cv_out, cmixed_out, clse_out, across_out, third_out) = kept[INSIDE:]
+    (before_ref, flat_ref, hot_ref, mask_ref, tiles_ref, weight_ref,
+     send_sem, recv_sem, own_sem, side_send, side_recv, keep_sem) = refs[2 * ARRAYS + 35 + INSIDE :]
     steps = len(bits)
     place = coords(bits)
     seq_pos = lax.axis_index("seq")
     rows = hidden_ref.shape[0]
     keys = first_out.shape[0]
     lanes = hidden_ref.shape[1] // (H // PAIR)
+
+    def kept_copy(number):
+        final = finals[number] if number < INSIDE else finals[number - INSIDE + ARRAYS]
+        return pltpu.make_async_copy(kept[number], final, keep_sem.at[number])
+
+    def keep(*numbers):
+        for number in numbers:
+            kept_copy(number).start()
+
+    def keep_act(*numbers):
+        keep(*(number + INSIDE for number in numbers))
 
     def own(array):
         return pltpu.make_async_copy(
@@ -538,6 +551,8 @@
 
     def arrived(item):
         copy(item, steps - 1).wait_recv()
+        if item < INSIDE:
+            keep(item)
 
     def side(which):
         source, target = ((hidden_ref, before_ref), (enc_ref, enc_out.at[rows:]))[which]
@@ -566,6 +581,7 @@
         own(array).start()
     greet(bits)
     enc_out[:rows, :] = enc_ref[...]
+    make_hot(buckets_ref, hot_ref, mask_ref)
     advance(STAGE_GAIN)
     arrived(0)
     gains = [gain_row(outs[0][...], gain_size, row) for row in range(3)]
@@ -598,6 +614,7 @@
     advance(STAGE_QUERY)
     arrived(1)
     project(1, first_out, q_out, rows, rows)
+    keep_act(2)
     advance(STAGE_KEY)
     side(0).wait_recv()
 
@@ -611,9 +628,11 @@
 
     arrived(2)
     project(2, first_out, k_out, 0, keys)
+    keep_act(1, 3)
     advance(STAGE_VALUE)
     arrived(3)
     project(3, first_out, v_out, 0, keys)
+    keep_act(4)
 
     advance(STAGE_SELF)
 
@@ -662,19 +681,24 @@
 
         over_rows(rows, body)
 
+    keep_act(5, 6)
     advance(STAGE_OUT)
     arrived(4)
     residual(4, mixed_out, hidden_ref, after_out, second_out, gains[1])
+    keep_act(7, 8)
     advance(STAGE_CQUERY)
     arrived(5)
     project(5, second_out, cq_out, 0, rows)
+    keep_act(9)
     advance(STAGE_CKEY)
     side(1).wait_recv()
     arrived(6)
     project(6, enc_out, ck_out, 0, keys)
+    keep_act(0, 10)
     advance(STAGE_CVALUE)
     arrived(7)
     project(7, enc_out, cv_out, 0, keys)
+    keep_act(11)
     advance(STAGE_CROSS)
 
     @pl.loop(0, H // PAIR)
@@ -688,10 +712,13 @@
             )
         between(pair, STAGE_CROSS)
 
-    advance(1000)
-
+    keep_act(12, 13)
+    advance(STAGE_COUT)
     arrived(8)
     residual(8, cmixed_out, after_out, across_out, third_out, gains[2])
+    keep_act(14, 15)
+    advance(STAGE_END)
+    assert not todo
     for item in range(INSIDE, ITEMS):
         arrived(item)
     for item in range(ITEMS):
@@ -699,9 +726,25 @@
             copy(item, step).wait_send()
     for which in range(2):
         side(which).wait_send()
-
-
-def open_layer(items, hidden, encoded, hot, mask, sizes, collective_id):
+    for number in range(len(kept)):
+        kept_copy(number).wait()
+
+
+def make_hot(buckets_ref, hot_ref, mask_ref):
+    offs, marks, width = hot_ref.shape
+    bucket = buckets_ref[...].astype(F32)
+    mark = lax.broadcasted_iota(jnp.int32, (marks, bucket.shape[1]), 0).astype(F32)
+    begin = jnp.sum((bucket < mark).astype(F32), 1, keepdims=True)
+    end = jnp.sum((bucket <= mark).astype(F32), 1, keepdims=True)
+    place = lax.broadcasted_iota(jnp.int32, (marks, width), 1).astype(F32)
+    step = jnp.where(place < TILE, place, place - width)
+    for off in range(offs):
+        gap = step + off * TILE
+        hot_ref[off] = ((gap >= begin) & (gap < end)).astype(F32).astype(LOW)
+        mask_ref[off] = jnp.where(gap[:1] >= 0, 0.0, NEGATIVE)
+
+
+def open_layer(items, hidden, encoded, buckets, sizes, collective_id):
     bits = bit_plan()
     steps = len(bits)
     count, width = hidden.shape
@@ -719,11 +762,14 @@
     outs = pl.pallas_call(
         functools.partial(open_kernel, bits, sizes),
         out_shape=[jax.ShapeDtypeStruct(*x) for x in shapes],
-        in_specs=[inside] * (ARRAYS + 4),
-        out_specs=[inside] * INSIDE + [outside] * (ARRAYS - INSIDE) + [inside] * 16,
-        scratch_shapes=[
+        in_specs=[inside] * (ARRAYS + 3),
+        out_specs=[outside] * (ARRAYS + 16),
+        scratch_shapes=[pltpu.VMEM(*x) for x in shapes[:INSIDE] + shapes[ARRAYS:]]
+        + [
             pltpu.VMEM((count, width), LOW),
             pltpu.VMEM((H * BUCKETS, 128), F32),
+            pltpu.VMEM((offs, BUCKETS, 2 * TILE), LOW),
+            pltpu.VMEM((offs, 1, 2 * TILE), F32),
             pltpu.VMEM((PAIR, offs, TILE, TILE), F32),
             pltpu.VMEM((width, width), LOW),
             sems,
@@ -731,12 +777,13 @@
             pltpu.SemaphoreType.DMA((ARRAYS,)),
             pltpu.SemaphoreType.DMA((2,)),
             pltpu.SemaphoreType.DMA((2,)),
+            pltpu.SemaphoreType.DMA((INSIDE + 16,)),
         ],
         compiler_params=pltpu.CompilerParams(
             collective_id=collective_id, has_side_effects=True, vmem_limit_bytes=66_000_000
         ),
         name="open_layer",
-    )(*items, hidden, encoded, hot, mask)
+    )(*items, hidden, encoded, buckets)
     return [out.reshape((-1,) + x.shape[-2:]) for out, x in zip(outs, items)] + list(outs[ARRAYS:])
 
 
@@ -746,13 +793,14 @@
 
 def close_kernel(bits, sizes, *refs):
     gain_size, table_size = sizes
-    (ff_refs, weights, cross_refs, self_refs, (smalls_ref, hot_ref, mask_ref, hidden_in),
-     (layer_out, hidden_out, enc_out), outs, (small_out,)) = take(refs, (7, 8, 7, 6, 4, 3, 11, 1))
-    rest = refs[47:]
+    (ff_refs, weights, cross_refs, self_refs, (smalls_ref, buckets_ref, hidden_in),
+     (layer_out, hidden_out, enc_out), outs, (small_out,)) = take(refs, (7, 8, 7, 6, 3, 3, 11, 1))
+    rest = refs[46:]
     arrivals = rest[: CLOSE_ITEMS * len(bits)]
     (work_ref, ff_work, down_work, small_ref, q_buf, k_buf, pair_buf, rows_buf, grad_buf,
      res_buf, after_buf, weight_buf, enc_own, send_buf, recv_buf, dk_acc, dv_acc,
-     tiles_ref, total_ref, rows_ref, flat_ref, gain_sums, send_sem, recv_sem, side_send, side_recv,
+     tiles_ref, total_ref, rows_ref, flat_ref, gain_sums, hot_ref,
+     mask_ref, send_sem, recv_sem, side_send, side_recv,
      fetch_sem) = rest[CLOSE_ITEMS * len(bits) :]
     steps = len(bits)
     place = coords(bits)
@@ -974,6 +1022,7 @@
         one.start()
     for one in loads:
         one.start()
+    make_hot(buckets_ref, hot_ref, mask_ref)
     greet(bits)
     flat_ref[...] = table_rows(smalls_ref[...], table_size, 3)
     gain_one, gain_two, gain_three = [gain_row(smalls_ref[...], gain_size, row) for row in range(3)]
@@ -1302,7 +1351,7 @@
 )
 
 
-def close_layer(forward, weights, cross, own, smalls, hot, mask, hidden, sizes, collective_id):
+def close_layer(forward, weights, cross, own, smalls, buckets, hidden, sizes, collective_id):
     bits = bit_plan()
     steps = len(bits)
     owners = 1 << steps
@@ -1334,7 +1383,7 @@
         + [jax.ShapeDtypeStruct(square, F32)] * 8
         + [jax.ShapeDtypeStruct((8, 128), F32)],
         in_specs=[outside] * (7 + 8) + [outside] * 6 + [inside] + [outside] * 5 + [inside]
-        + [inside] * 3 + [outside],
+        + [inside] * 2 + [outside],
         out_specs=[outside, inside, outside] + [inside] * 12,
         scratch_shapes=arrivals
         + [
@@ -1348,13 +1397,14 @@
             vm((length, lanes), F32), vm((length, lanes), F32),
             vm((PAIR, offs, TILE, TILE), F32), vm((PAIR, offs, TILE, TILE), F32),
             vm((H * BUCKETS, 128), F32), vm((H * BUCKETS, 128), F32), vm((8, width), F32),
+            vm((offs, BUCKETS, 2 * TILE), LOW), vm((offs, 1, 2 * TILE), F32),
             sems, sems, pair_sem, pair_sem, pltpu.SemaphoreType.DMA((16,)),
         ],
         compiler_params=pltpu.CompilerParams(
             collective_id=collective_id, has_side_effects=True, vmem_limit_bytes=67_000_000
         ),
         name="close_layer",
-    )(*forward, *weights, *cross, *own, smalls, hot, mask, hidden)
+    )(*forward, *weights, *cross, *own, smalls, buckets, hidden)
 
 
 def finish_kernel(*refs):
@@ -1403,10 +1453,11 @@
     return jax.nn.gelu(gate, approximate=True) * upper
 
 
-def pad_rows(rows, dtype):
-    return jnp.stack([jnp.pad(row.astype(dtype), (0, 128 - row.shape[0])) for row in rows] + [
-        jnp.zeros((128,), dtype)
-    ] * (8 - len(rows)))
+def pad_rows(rows):
+    return sum(
+        jnp.pad(row.astype(F32)[None], ((place, 7 - place), (0, 128 - row.shape[0])))
+        for place, row in enumerate(rows)
+    )
 
 
 def on_device(
@@ -1438,20 +1489,17 @@
     width = hidden_in.shape[2]
     own_low = hidden_in[0]
     enc_own = encoded[0]
-    small = pad_rows([norm_self, norm_cross, norm_ff, bias_table], F32)
+    small = pad_rows([norm_self, norm_cross, norm_ff, bias_table])
     hidden = own_low.astype(F32)
     count = hidden.shape[0]
     length = count * lax.axis_size("seq")
     gap, hot = bucket_rows(buckets, length)
-    hot_rows = jnp.swapaxes(hot, 0, 1)
-    hot_mask = jnp.where(gap >= 0, 0.0, NEGATIVE)[:, None, :]
     opened = open_layer(
         [small, self_query, self_key, self_value, self_out, cross_query, cross_key, cross_value,
          cross_out, ff_gate, ff_up, ff_down],
         own_low,
         enc_own,
-        hot_rows,
-        hot_mask,
+        buckets.reshape(1, -1),
         (norm_self.shape[0], bias_table.shape[0]),
         1,
     )
@@ -1477,8 +1525,7 @@
             [cross_q, cross_k, cross_v, cross_mixed, enc_all, second, cross_lse],
             [query, key, value, self_mixed, first_all, self_lse],
             smalls,
-            hot_rows,
-            hot_mask,
+            buckets.reshape(1, -1),
             own_low,
             (gains, bias_table.shape[0]),
             2,

time: 257 us -> 247 us (0.961)
  Pallas kernels: 249 us -> 242 us
    pallas_call x1, Pallas kernels: 107 us -> 99.9 us  [open_layer(): pl.pallas_call(functools.partial(open_kernel, bits, sizes), out_shape=[ja...]
where the time goes in v1:
time: 247 us; the launch traced here: 244 us
  Pallas kernels  242 us (98%)
    pallas_call x1, Pallas kernels, close_layer(): pl.pallas_call(functools.partial(close_kernel, bits, sizes), out_shape=[j...  138 us
    pallas_call x1, Pallas kernels, open_layer(): pl.pallas_call(functools.partial(open_kernel, bits, sizes), out_shape=[ja...  99.9 us

profile of v1, /device:TPU:0, one launch (start us, length us, event | category | flops | bytes accessed | tf_op | source)
XLA Modules:
  0.0 244.5 jit_solution(7965048057836620103)
XLA Ops:
  0.7 1.3 convert_add_fusion.refs_0_
  2.0 99.9 %open_layer.1 = (f32[2,2,2,2,2,8,128]{6,5,4,3,2,1,0:T(8,128)}, bf16[2,2,2,2,2,24,768]{6,5,4,3,2,1,0:T(8,128)(2,1)}, bf16[2,2,2,2,2,24,768]{6,5,4,3,2,1,0:T(8,128...) custom-call(f32[8,128]{1,0:T(8,128)} %convert_add_fusion.refs_0_, ...), custom_call_target="tpu_custom_call" | custom-call | tf_op jit(solution)/shard_map/open_layer/pallas_call | solution.py:762
  101.9 138.3 %close_layer.1 = (bf16[512,768]{1,0:T(8,128)(2,1)}, bf16[512,768]{1,0:T(8,128)(2,1)}, bf16[512,768]{1,0:T(8,128)(2,1)}, f32[24,2048]{1,0:T(8,128)}, f32[24,2048]...) custom-call(bf16[512,768]{1,0:T(8,128)(2,1)} %get-tuple-element.79.r, ...), custom_call_target="tpu_custom_call" | custom-call | tf_op jit(solution)/shard_map/close_layer/pallas_call | solution.py:1379
  240.2 3.8 %finish.1 = (bf16[512,768]{1,0:T(8,128)(2,1)}, bf16[512,768]{1,0:T(8,128)(2,1)}, bf16[512,768]{1,0:T(8,128)(2,1)}, f32[24,2048]{1,0:T(8,128)}, f32[24,2048]{1,0:...) custom-call(bf16[512,768]{1,0:T(8,128)(2,1)} %get-tuple-element.107., ...), custom_call_target="tpu_custom_call" | custom-call | tf_op jit(solution)/shard_map/finish/pallas_call | solution.py:1422

commit v2 on v1

--- a/solution.py
+++ b/solution.py
@@ -862,6 +862,8 @@
                 mine = arrival(item, step - 1)[here]
             else:
                 mine = base(item)[here + part_of(item)]
+            if free:
+                return mine + target[tuple(sub)]
             return mine.astype(F32) + target[tuple(sub)].astype(F32)
 
         if not free:
@@ -876,10 +878,19 @@
                 outs[item - SQUARES + 3][...] = one(())
             return
 
-        @pl.loop(0, 1 << len(free))
+        outer = max(0, len(free) - 2)
+
+        def several(sub):
+            sub = tuple(sub) + (slice(None),) * (len(free) - outer)
+            target[sub] = one(sub)
+
+        if outer == 0:
+            several(())
+            return
+
+        @pl.loop(0, 1 << outer)
         def _(index):
-            sub = [lax.rem(index // (1 << (len(free) - 1 - i)), 2) for i in range(len(free))]
-            target[tuple(sub)] = one(sub).astype(target.dtype)
+            several([lax.rem(index // (1 << (outer - 1 - i)), 2) for i in range(outer)])
 
     def side(which):
         return remote(

time: 247 us -> 241 us (0.976)
  Pallas kernels: 242 us -> 236 us
    pallas_call x1, Pallas kernels: 138 us -> 133 us  [close_layer(): pl.pallas_call(functools.partial(close_kernel, bits, sizes), out_shape=[j...]
where the time goes in v2:
time: 241 us; the launch traced here: 239 us
  Pallas kernels  236 us (98%)
    pallas_call x1, Pallas kernels, close_layer(): pl.pallas_call(functools.partial(close_kernel, bits, sizes), out_shape=[j...  133 us
    pallas_call x1, Pallas kernels, open_layer(): pl.pallas_call(functools.partial(open_kernel, bits, sizes), out_shape=[ja...  99.9 us

profile of v2, /device:TPU:0, one launch (start us, length us, event | category | flops | bytes accessed | tf_op | source)
XLA Modules:
  0.0 238.7 jit_solution(7356333225072497039)
XLA Ops:
  0.7 1.3 convert_add_fusion.refs_0_
  2.0 99.9 %open_layer.1 = (f32[2,2,2,2,2,8,128]{6,5,4,3,2,1,0:T(8,128)}, bf16[2,2,2,2,2,24,768]{6,5,4,3,2,1,0:T(8,128)(2,1)}, bf16[2,2,2,2,2,24,768]{6,5,4,3,2,1,0:T(8,128...) custom-call(f32[8,128]{1,0:T(8,128)} %convert_add_fusion.refs_0_, ...), custom_call_target="tpu_custom_call" | custom-call | tf_op jit(solution)/shard_map/open_layer/pallas_call | solution.py:762
  101.9 132.5 %close_layer.1 = (bf16[512,768]{1,0:T(8,128)(2,1)}, bf16[512,768]{1,0:T(8,128)(2,1)}, bf16[512,768]{1,0:T(8,128)(2,1)}, f32[24,2048]{1,0:T(8,128)}, f32[24,2048]...) custom-call(bf16[512,768]{1,0:T(8,128)(2,1)} %get-tuple-element.79.r, ...), custom_call_target="tpu_custom_call" | custom-call | tf_op jit(solution)/shard_map/close_layer/pallas_call | solution.py:1390
  234.4 3.8 %finish.1 = (bf16[512,768]{1,0:T(8,128)(2,1)}, bf16[512,768]{1,0:T(8,128)(2,1)}, bf16[512,768]{1,0:T(8,128)(2,1)}, f32[24,2048]{1,0:T(8,128)}, f32[24,2048]{1,0:...) custom-call(bf16[512,768]{1,0:T(8,128)(2,1)} %get-tuple-element.107., ...), custom_call_target="tpu_custom_call" | custom-call | tf_op jit(solution)/shard_map/finish/pallas_call | solution.py:1433

commit v3 on v2

--- a/solution.py
+++ b/solution.py
@@ -878,7 +878,7 @@
                 outs[item - SQUARES + 3][...] = one(())
             return
 
-        outer = max(0, len(free) - 2)
+        outer = max(0, len(free) - 3)
 
         def several(sub):
             sub = tuple(sub) + (slice(None),) * (len(free) - outer)

time: 241 us -> 241 us (level)
  no operation moved by 1% of the time
where the time goes in v3:
time: 241 us; the launch traced here: 238 us
  Pallas kernels  236 us (98%)
    pallas_call x1, Pallas kernels, close_layer(): pl.pallas_call(functools.partial(close_kernel, bits, sizes), out_shape=[j...  132 us
    pallas_call x1, Pallas kernels, open_layer(): pl.pallas_call(functools.partial(open_kernel, bits, sizes), out_shape=[ja...  99.9 us

profile of v3, /device:TPU:0, one launch (start us, length us, event | category | flops | bytes accessed | tf_op | source)
XLA Modules:
  0.0 238.2 jit_solution(1169922314623458054)
XLA Ops:
  0.7 1.3 convert_add_fusion.refs_0_
  2.0 99.9 %open_layer.1 = (f32[2,2,2,2,2,8,128]{6,5,4,3,2,1,0:T(8,128)}, bf16[2,2,2,2,2,24,768]{6,5,4,3,2,1,0:T(8,128)(2,1)}, bf16[2,2,2,2,2,24,768]{6,5,4,3,2,1,0:T(8,128...) custom-call(f32[8,128]{1,0:T(8,128)} %convert_add_fusion.refs_0_, ...), custom_call_target="tpu_custom_call" | custom-call | tf_op jit(solution)/shard_map/open_layer/pallas_call | solution.py:762
  101.9 132.0 %close_layer.1 = (bf16[512,768]{1,0:T(8,128)(2,1)}, bf16[512,768]{1,0:T(8,128)(2,1)}, bf16[512,768]{1,0:T(8,128)(2,1)}, f32[24,2048]{1,0:T(8,128)}, f32[24,2048]...) custom-call(bf16[512,768]{1,0:T(8,128)(2,1)} %get-tuple-element.79.r, ...), custom_call_target="tpu_custom_call" | custom-call | tf_op jit(solution)/shard_map/close_layer/pallas_call | solution.py:1390
  233.9 3.8 %finish.1 = (bf16[512,768]{1,0:T(8,128)(2,1)}, bf16[512,768]{1,0:T(8,128)(2,1)}, bf16[512,768]{1,0:T(8,128)(2,1)}, f32[24,2048]{1,0:T(8,128)}, f32[24,2048]{1,0:...) custom-call(bf16[512,768]{1,0:T(8,128)(2,1)} %get-tuple-element.107., ...), custom_call_target="tpu_custom_call" | custom-call | tf_op jit(solution)/shard_map/finish/pallas_call | solution.py:1433
